TPU v7x, 32 devices: a whole 2x2x4 slice. The times are simulated.
32 devices in a mesh: dp: 4 (over z), vocab: 8 (over y, x, core).
Axes of the slice: x: 2, y: 2, z: 4, core: 2. Of those that a mesh axis runs over, the one named last changes fastest.
Arguments:
- hidden: bfloat16 [32, 14, 4096], P('dp', None, 'vocab'), may hold values from -400 to 400
- weight: bfloat16 [4096, 16032], P(None, ('dp', 'vocab')), may hold values from -0.09375 to 0.09375
- targets: int32 [32, 14], P('dp'), may hold values from 0 to 16031
- lengths: int32 [4, 8], P('dp'), may hold values from 1 to 14, 56 in all within a row
- rewards: int32 [4, 8], P('dp'), may hold values from -256 to 256
- arrival: int32 [32], replicated, may hold values from 0 to 31, each once
Outputs:
- token_logprobs: float32 [32, 14], P('dp')
- advantages: float32 [32], P('dp')
- weighted: float32 [32], P('dp')
Inputs may be any that keep to these rules, and one draw needn't show every extreme that they name: The lengths of one device's 8 completions sum to exactly 56, and one of them is 14. `arrival`: every completion number appears once; completion p * 8 + j is sample j of prompt p.
All inputs are finite; a program needn't handle non-finite values.
Results may differ from a plain program's by a relative error of at most 0.0003.
Values may be sent and summed in bfloat16 or wider, within the bound.
A program may use at most 192 MiB of HBM per device.

v0:
```python
import jax
import jax.numpy as jnp
from jax import lax
from jax.sharding import PartitionSpec as P

SAMPLES = 8
reward_unit = 1.0 / 64.0


def combined_all(value, axis, join):
    pieces = jax.tree.map(lambda part: lax.all_gather(part, axis), value)
    head = jax.tree.map(lambda part: part[0], pieces)
    tail = jax.tree.map(lambda part: part[1:], pieces)
    subtotal, _ = lax.scan(lambda subtotal, share: (join(subtotal, share), None), head, tail)
    return subtotal


def merge_totals(first, second):
    highest = jnp.maximum(first[0], second[0])
    totals = first[1] * jnp.exp(first[0] - highest) + second[1] * jnp.exp(second[0] - highest)
    return (highest, totals, first[2] + second[2])


def local(hidden, weight, targets, lengths, rewards, arrival):
    dp_count = lax.axis_size("dp")
    vocab_count = lax.axis_size("vocab")
    per_device = hidden.shape[0]
    window = hidden.shape[1]
    shard_width = weight.shape[1]
    completions = per_device * dp_count
    owner = lax.axis_index("dp")
    first_column = (owner * vocab_count + lax.axis_index("vocab")) * shard_width
    all_lengths, all_rewards = (
        lax.all_gather(lengths, "dp", axis=0, tiled=True),
        lax.all_gather(rewards, "dp", axis=0, tiled=True),
    )
    features = lax.all_gather(hidden, "vocab", axis=2, tiled=True)
    model_width = features.shape[2]
    column_ids = lax.iota(jnp.int32, shard_width)
    position_ids = lax.iota(jnp.int32, window)
    slot_ids = lax.iota(jnp.int32, completions)
    matching = arrival[None, :] == slot_ids[:, None]

    def lookup(table):
        return jnp.sum(jnp.where(matching, table[None, :], 0), axis=1)

    slot_of = lookup(slot_ids)
    length_of = lookup(all_lengths.reshape(completions))
    reward_of = lookup(all_rewards.reshape(completions)).astype(jnp.float32) * reward_unit
    shard_part = (
        lax.all_gather(features, "dp", axis=0, tiled=True),
        lax.all_gather(targets, "dp", axis=0, tiled=True),
    )
    count = shard_part[0].shape[0] * window
    row_block = shard_part[0].reshape(count, model_width)
    logits = jnp.dot(row_block, weight, preferred_element_type=jnp.float32)
    highest = jnp.max(logits, axis=1)
    totals = jnp.sum(jnp.exp(logits - highest[:, None]), axis=1)
    local_ids = shard_part[1].reshape(count) - first_column
    picked = jnp.sum(jnp.where(column_ids[None, :] == local_ids[:, None], logits, 0.0), axis=1)
    stats = (highest, totals, picked)
    stats = (stats[0], stats[1], stats[2])
    base_of = slot_of * window
    usable = position_ids[None, :] < length_of[:, None]
    source_rows = jnp.where(usable, base_of[:, None] + position_ids[None, :], 0)
    my_usable = lax.dynamic_slice_in_dim(usable, owner * per_device, per_device, 0)
    ordered_high = stats[0][source_rows].reshape(dp_count, per_device * window)
    ordered_totals = stats[1][source_rows].reshape(dp_count, per_device * window)
    ordered_picked = stats[2][source_rows].reshape(dp_count, per_device * window)
    arrived = (
        lax.all_to_all(ordered_high, "dp", split_axis=0, concat_axis=0, tiled=True),
        lax.all_to_all(ordered_totals, "dp", split_axis=0, concat_axis=0, tiled=True),
        lax.all_to_all(ordered_picked, "dp", split_axis=0, concat_axis=0, tiled=True),
    )
    highest = jnp.max(arrived[0], axis=0)
    totals = jnp.sum(arrived[1] * jnp.exp(arrived[0] - highest[None, :]), axis=0)
    picked = jnp.sum(arrived[2], axis=0)
    highest, totals, picked = combined_all((highest, totals, picked), "vocab", merge_totals)
    highest = highest.reshape(per_device, window)
    totals = totals.reshape(per_device, window)
    picked = picked.reshape(per_device, window)
    token_logprobs = jnp.where(my_usable, picked - highest - jnp.log(totals), 0.0)
    my_rewards = lax.dynamic_slice_in_dim(reward_of, owner * per_device, per_device, 0)
    my_lengths = lax.dynamic_slice_in_dim(length_of, owner * per_device, per_device, 0)
    groups = jnp.sum(my_rewards.reshape(per_device // SAMPLES, SAMPLES), axis=1)
    advantages = my_rewards - (jnp.repeat(groups, SAMPLES) - my_rewards) / (SAMPLES - 1.0)
    weighted = advantages * jnp.sum(token_logprobs, axis=1) / my_lengths.astype(jnp.float32)
    return (token_logprobs, advantages, weighted)


def solution(mesh):
    return jax.shard_map(
        local,
        mesh=mesh,
        in_specs=(
            P("dp", None, "vocab"),
            P(None, ("dp", "vocab")),
            P("dp", None),
            P("dp", None),
            P("dp", None),
            P(),
        ),
        out_specs=(P("dp", None), P("dp"), P("dp")),
        check_vma=False,
    )
```

profile of v0, /device:TPU:0, one launch (start us, length us, event | category | flops | bytes accessed | tf_op | source)
XLA Modules:
  0.0 175.6 jit_solution(2976874843851512155)
XLA Ops:
  7.2 14.2 %all_gather.34 = bf16[8,14,4096]{2,0,1:T(8,128)(2,1)} all-gather(bf16[8,14,512]{2,0,1:T(8,128)(2,1)} %param.8), channel_id=1, replica_groups=mesh['dp'=4,'vocab'=8] {'vocab'}, dimensions={2}, use_global_device_ids=true | all-gather | bytes 1032192 | tf_op jit(solution)/shard_map/all_gather | solution.py:37
  21.4 11.3 %all-gather.4 = s32[4,1,8]{2,1,0:T(1,128)S(1)} all-gather(s32[1,1,8]{2,1,0:T(1,128)} %bitcast.32), channel_id=1, replica_groups=mesh['dp'=4,'vocab'=8] {'dp'}, dimensions={0}, use_global_device_ids=true | all-gather | bytes 160 | tf_op jit(solution)/shard_map/all_gather | solution.py:35
  32.7 8.2 %all-gather.3 = s32[4,1,8]{2,1,0:T(1,128)S(1)} all-gather(s32[1,1,8]{2,1,0:T(1,128)} %bitcast.33), channel_id=1, replica_groups=mesh['dp'=4,'vocab'=8] {'dp'}, dimensions={0}, use_global_device_ids=true | all-gather | bytes 160 | tf_op jit(solution)/shard_map/all_gather | solution.py:34
  41.4 0.7 reduce.11
  42.2 0.7 reduce.10
  42.9 0.8 select_reduce_fusion.1
  43.9 14.1 %all_gather.40 = s32[32,14]{1,0:T(8,128)S(1)} all-gather(s32[8,14]{1,0:T(8,128)} %param.10), channel_id=1, replica_groups=mesh['dp'=4,'vocab'=8] {'dp'}, dimensions={0}, use_global_device_ids=true | all-gather | bytes 2240 | tf_op jit(solution)/shard_map/all_gather | solution.py:52
  58.1 36.0 %all-gather.7.cloned.1.call-done = bf16[32,14,4096]{2,0,1:T(8,128)(2,1)} async-done(((bf16[8,14,4096]{2,0,1:T(8,128)(2,1)}), bf16[32,14,4096]{2,0,1:T(8,128)(2,1)}) %all-gather.7.cloned.1.call-update) | async-done | bytes 3670032 | tf_op jit(solution)/shard_map/all_gather | solution.py:51
  94.1 6.0 %copy.13 = bf16[32,14,4096]{2,1,0:T(8,128)(2,1)} copy(bf16[32,14,4096]{2,0,1:T(8,128)(2,1)} %all-gather.7.cloned.1.call-done) | data formatting | bytes 7340032 | tf_op jit(solution)/shard_map/all_gather | solution.py:51
  100.1 5.0 %reshape.122 = bf16[448,4096]{1,0:T(8,128)(2,1)} reshape(bf16[32,14,4096]{2,1,0:T(8,128)(2,1)} %copy.13) | data formatting | bytes 7340032 | tf_op jit(solution)/shard_map/reshape | solution.py:55
  105.1 5.5 %fusion.11 = (f32[448]{0:T(512)S(1)}, f32[448,501]{1,0:T(8,128)S(1)}) fusion(bf16[448,4096]{1,0:T(8,128)(2,1)} %reshape.122, bf16[4096,501]{0,1:T(8,128)(2,1)} %param.9), kind=kOutput, calls=%fused_computation.34 | convolution fusion | flops 1838902016 | bytes 8673792 | tf_op jit(solution)/shard_map/dot_general | solution.py:56
  110.5 3.1 %gather_fusion = f32[448]{0:T(512)S(1)} fusion(f32[448]{0:T(512)S(1)} %get-tuple-element.74, s32[1024]{0:T(1024)S(1)} %pad_clamp_fusion), kind=kCustom, calls=%fused_computation | custom fusion | bytes 5376 | tf_op jit(solution)/shard_map/gather | solution.py:67
  114.4 3.2 %all-to-all-start = ((f32[4,1,112]{2,1,0:T(1,128)}), f32[4,1,112]{2,1,0:T(1,128)S(1)}, u32[]{:S(2)}, u32[]{:S(2)}) async-start(f32[4,1,112]{2,1,0:T(1,128)} %all_to_all.22), calls=%async_computation | async-start | bytes 4096 | tf_op jit(solution)/shard_map/all_to_all | solution.py:71
  118.1 3.1 %gather_fusion.1 = f32[448]{0:T(512)S(1)} fusion(f32[448]{0:T(512)S(1)} %get-tuple-element.46, s32[1024]{0:T(1024)S(1)} %pad_clamp_fusion), kind=kCustom, calls=%fused_computation.1 | custom fusion | bytes 5376 | tf_op jit(solution)/shard_map/gather | solution.py:68
  121.2 0.7 all_to_all.24
  121.9 1.1 all-to-all-done
  123.1 3.9 %all-to-all-start.1 = ((f32[4,1,112]{2,1,0:T(1,128)}), f32[4,1,112]{2,1,0:T(1,128)S(1)}, u32[]{:S(2)}, u32[]{:S(2)}) async-start(f32[4,1,112]{2,1,0:T(1,128)} %all_to_all.24), calls=%async_computation.1 | async-start | bytes 4096 | tf_op jit(solution)/shard_map/all_to_all | solution.py:72
  127.0 0.7 dynamic-slice_reduce_fusion
  128.9 3.1 %gather_fusion.2 = f32[448]{0:T(512)S(1)} fusion(f32[448]{0:T(512)S(1)} %get-tuple-element.45, s32[1024]{0:T(1024)S(1)} %pad_clamp_fusion), kind=kCustom, calls=%fused_computation.2 | custom fusion | bytes 5376 | tf_op jit(solution)/shard_map/gather | solution.py:69
  132.8 5.1 %all-to-all-start.2 = ((f32[4,1,112]{2,1,0:T(1,128)}), f32[4,1,112]{2,1,0:T(1,128)S(1)}, u32[]{:S(2)}, u32[]{:S(2)}) async-start(f32[4,1,112]{2,1,0:T(1,128)} %all_to_all.28), calls=%async_computation.2 | async-start | bytes 4096 | tf_op jit(solution)/shard_map/all_to_all | solution.py:73
  138.4 5.0 %all-to-all-done.2 = f32[4,1,112]{2,1,0:T(1,128)S(1)} async-done(((f32[4,1,112]{2,1,0:T(1,128)}), f32[4,1,112]{2,1,0:T(1,128)S(1)}, u32[]{:S(2)}, u32[]{:S(2)}) %all-to-all-start.2) | async-done | bytes 1824 | tf_op jit(solution)/shard_map/all_to_all | solution.py:73
  143.7 22.3 %all-reduce.3 = (f32[896]{0:T(1024)S(1)}, f32[896]{0:T(1024)S(1)}, f32[896]{0:T(1024)S(1)}) all-reduce(f32[896]{0:T(1024)S(1)} %dynamic-update-slice, f32[896]{0:T(1024)S(1)} %dynamic-update-slice.1, f32[896]{0:T(1024)S(1)} %dynamic-update-slice.2), channel_id=2, replica_groups=mesh['dp'=4,'vocab'=8] {'vocab'}, use_global_device_ids=true, to_apply=%add | all-reduce | flops 2688 | bytes 21504
  166.8 0.8 fusion.9
  167.6 1.2 convert_divide_fusion
  (48 shorter events, 5.3 us)
Async XLA Ops:
  7.2 87.0 %all-gather.7.cloned.1.call-start = ((), (), s32[]{:S(2)}) async-start(), calls=%async_computation.3 | async-start | bytes 4587520 | tf_op jit(solution)/shard_map/all_gather | solution.py:51
  114.4 8.7 %all-to-all-start = ((f32[4,1,112]{2,1,0:T(1,128)}), f32[4,1,112]{2,1,0:T(1,128)S(1)}, u32[]{:S(2)}, u32[]{:S(2)}) async-start(f32[4,1,112]{2,1,0:T(1,128)} %all_to_all.22), calls=%async_computation | async-start | bytes 4096 | tf_op jit(solution)/shard_map/all_to_all | solution.py:71
  118.1 9.6 %copy-start = (u32[32]{0:T(128)S(1)}, u32[32]{0:T(128)}, u32[]{:S(2)}) copy-start(u32[32]{0:T(128)} %constant.44) | copy-start | bytes 388
  123.1 9.7 %all-to-all-start.1 = ((f32[4,1,112]{2,1,0:T(1,128)}), f32[4,1,112]{2,1,0:T(1,128)S(1)}, u32[]{:S(2)}, u32[]{:S(2)}) async-start(f32[4,1,112]{2,1,0:T(1,128)} %all_to_all.24), calls=%async_computation.1 | async-start | bytes 4096 | tf_op jit(solution)/shard_map/all_to_all | solution.py:72
  132.8 10.6 %all-to-all-start.2 = ((f32[4,1,112]{2,1,0:T(1,128)}), f32[4,1,112]{2,1,0:T(1,128)S(1)}, u32[]{:S(2)}, u32[]{:S(2)}) async-start(f32[4,1,112]{2,1,0:T(1,128)} %all_to_all.28), calls=%async_computation.2 | async-start | bytes 4096 | tf_op jit(solution)/shard_map/all_to_all | solution.py:73
Sparse Core Ops, SparseCore 0:
  21.5 72.5 all-gather.6
where the time goes:
time: 176 us
  blocking collectives  70.1 us (40%)
  waiting for transfers between devices  42.2 us (24%)
  local copies, waits for them, and re-layouts  25.2 us (14%)
  between operations  14.8 us (8%)
  starting transfers between devices  12.3 us (7%)
  other arithmetic  5.56 us (3%)
  matrix products  5.47 us (3%)
    all_gather x1, waiting for transfers between devices, local(): lax.all_gather(features, 'dp', axis=0, tiled=True)  36 us
    unnamed x1, blocking collectives  22.3 us
    all_gather x1, blocking collectives, local(): features = lax.all_gather(hidden, 'vocab', axis=2, tiled=True)  14.2 us
    all_gather x1, blocking collectives, local(): lax.all_gather(targets, 'dp', axis=0, tiled=True)  14.1 us
    all_gather x1, blocking collectives, local(): lax.all_gather(rewards, 'dp', axis=0, tiled=True)  11.3 us
    all_gather x1, blocking collectives, local(): lax.all_gather(lengths, 'dp', axis=0, tiled=True)  8.2 us
    all_gather x1, local copies, waits for them, and re-layouts, local(): lax.all_gather(features, 'dp', axis=0, tiled=True)  5.99 us
    dot_general x1, matrix products, local(): logits = jnp.dot(row_block, weight, preferred_element_type=jnp.float32)  5.47 us
  transfers between devices with their start and end apart: 4, of which 3 were waited for; matrix products, arithmetic and copies ran while one was open for 7% of the time, Pallas kernels for 0%

commit v1 on v0

--- a/solution.py
+++ b/solution.py
@@ -34,7 +34,14 @@
         lax.all_gather(lengths, "dp", axis=0, tiled=True),
         lax.all_gather(rewards, "dp", axis=0, tiled=True),
     )
-    features = lax.all_gather(hidden, "vocab", axis=2, tiled=True)
+    ring = [hidden]
+    for hop in range(7):
+        ring.append(lax.ppermute(ring[-1], "vocab", [(dev, (dev + 1) % 8) for dev in range(8)]))
+    features = jnp.roll(
+        jnp.concatenate(ring[::-1], axis=2),
+        (lax.axis_index("vocab") + 1) * ring[0].shape[2],
+        axis=2,
+    )
     model_width = features.shape[2]
     column_ids = lax.iota(jnp.int32, shard_width)
     position_ids = lax.iota(jnp.int32, window)

time: 176 us -> 200 us (1.14)
  waiting for transfers between devices: 42.2 us -> 79.8 us
  blocking collectives: 70.1 us -> 56 us
  local copies, waits for them, and re-layouts: 25.2 us -> 27.3 us
    ppermute x0 -> x7, waiting for transfers between devices: none -> 36.2 us  [local(): lax.ppermute(ring[-1], 'vocab', [(dev, (dev + 1) % 8) for dev in range(8)])]
    all_gather x1 -> x0, blocking collectives: 14.2 us -> none  [local(): features = lax.all_gather(hidden, 'vocab', axis=2, tiled=True)]
    all_gather x1, blocking collectives: 8.2 us -> 11.9 us  [local(): lax.all_gather(lengths, 'dp', axis=0, tiled=True)]
    all_to_all x1, waiting for transfers between devices: 5.01 us -> 1.56 us  [local(): lax.all_to_all(ordered_picked, 'dp', split_axis=0, concat_axis=0, tiled=T...]
    all_gather x1, blocking collectives: 11.3 us -> 7.99 us  [local(): lax.all_gather(rewards, 'dp', axis=0, tiled=True)]
    all_to_all x1, waiting for transfers between devices: 0.01 us -> 2.89 us  [local(): lax.all_to_all(ordered_totals, 'dp', split_axis=0, concat_axis=0, tiled=T...]
  transfers between devices with their start and end apart: 4 -> 11, of which waited for: 3 -> 11; matrix products, arithmetic and copies ran while one was open for 7% -> 5% of each run, Pallas kernels for 0% -> 0%
where the time goes in v1:
time: 200 us; the launch traced here: 199 us
  waiting for transfers between devices  79.8 us (40%)
  blocking collectives  56 us (28%)
  local copies, waits for them, and re-layouts  27.3 us (14%)
  between operations  15 us (8%)
  starting transfers between devices  10.8 us (5%)
  matrix products  5.47 us (3%)
  other arithmetic  4.92 us (2%)
    all_gather x1, waiting for transfers between devices, local(): lax.all_gather(features, 'dp', axis=0, tiled=True)  37.4 us
    ppermute x7, waiting for transfers between devices, local(): lax.ppermute(ring[-1], 'vocab', [(dev, (dev + 1) % 8) for dev in range(8)])  36.2 us
    unnamed x1, blocking collectives  22.3 us
    all_gather x1, blocking collectives, local(): lax.all_gather(targets, 'dp', axis=0, tiled=True)  13.8 us
    all_gather x1, blocking collectives, local(): lax.all_gather(lengths, 'dp', axis=0, tiled=True)  11.9 us
    all_gather x1, blocking collectives, local(): lax.all_gather(rewards, 'dp', axis=0, tiled=True)  7.99 us
    all_gather x1, local copies, waits for them, and re-layouts, local(): lax.all_gather(features, 'dp', axis=0, tiled=True)  5.99 us
    dot_general x1, matrix products, local(): logits = jnp.dot(row_block, weight, preferred_element_type=jnp.float32)  5.47 us
  transfers between devices with their start and end apart: 11, of which 11 were waited for; matrix products, arithmetic and copies ran while one was open for 5% of the time, Pallas kernels for 0%

profile of v1, /device:TPU:0, one launch (start us, length us, event | category | flops | bytes accessed | tf_op | source)
XLA Modules:
  0.0 199.3 jit_solution(11706684218137407399)
XLA Ops:
  7.8 5.6 %collective-permute-done = bf16[8,14,512]{2,0,1:T(8,128)(2,1)S(1)} collective-permute-done((bf16[8,14,512]{2,0,1:T(8,128)(2,1)}, bf16[8,14,512]{2,0,1:T(8,128)(2,1)S(1)}, u32[]{:S(2)}, u32[]{:S(2)}) %collective-permute-start) | collective-permute-done | bytes 114720 | tf_op jit(solution)/shard_map/ppermute | solution.py:39
  13.3 5.1 %collective-permute-done.1 = bf16[8,14,512]{2,0,1:T(8,128)(2,1)S(1)} collective-permute-done((bf16[8,14,512]{2,0,1:T(8,128)(2,1)S(1)}, bf16[8,14,512]{2,0,1:T(8,128)(2,1)S(1)}, u32[]{:S(2)}, u32[]{:S(2)}) %collective-permute-start.1) | collective-permute-done | bytes 114720 | tf_op jit(solution)/shard_map/ppermute | solution.py:39
  18.4 5.1 %collective-permute-done.2 = bf16[8,14,512]{2,0,1:T(8,128)(2,1)S(1)} collective-permute-done((bf16[8,14,512]{2,0,1:T(8,128)(2,1)S(1)}, bf16[8,14,512]{2,0,1:T(8,128)(2,1)S(1)}, u32[]{:S(2)}, u32[]{:S(2)}) %collective-permute-start.2) | collective-permute-done | bytes 114720 | tf_op jit(solution)/shard_map/ppermute | solution.py:39
  23.6 5.1 %collective-permute-done.3 = bf16[8,14,512]{2,0,1:T(8,128)(2,1)S(1)} collective-permute-done((bf16[8,14,512]{2,0,1:T(8,128)(2,1)S(1)}, bf16[8,14,512]{2,0,1:T(8,128)(2,1)S(1)}, u32[]{:S(2)}, u32[]{:S(2)}) %collective-permute-start.3) | collective-permute-done | bytes 114720 | tf_op jit(solution)/shard_map/ppermute | solution.py:39
  28.7 5.1 %collective-permute-done.4 = bf16[8,14,512]{2,0,1:T(8,128)(2,1)S(1)} collective-permute-done((bf16[8,14,512]{2,0,1:T(8,128)(2,1)S(1)}, bf16[8,14,512]{2,0,1:T(8,128)(2,1)S(1)}, u32[]{:S(2)}, u32[]{:S(2)}) %collective-permute-start.4) | collective-permute-done | bytes 114720 | tf_op jit(solution)/shard_map/ppermute | solution.py:39
  33.8 5.1 %collective-permute-done.5 = bf16[8,14,512]{2,0,1:T(8,128)(2,1)S(1)} collective-permute-done((bf16[8,14,512]{2,0,1:T(8,128)(2,1)S(1)}, bf16[8,14,512]{2,0,1:T(8,128)(2,1)S(1)}, u32[]{:S(2)}, u32[]{:S(2)}) %collective-permute-start.5) | collective-permute-done | bytes 114720 | tf_op jit(solution)/shard_map/ppermute | solution.py:39
  38.9 5.1 %collective-permute-done.6 = bf16[8,14,512]{2,0,1:T(8,128)(2,1)S(1)} collective-permute-done((bf16[8,14,512]{2,0,1:T(8,128)(2,1)S(1)}, bf16[8,14,512]{2,0,1:T(8,128)(2,1)S(1)}, u32[]{:S(2)}, u32[]{:S(2)}) %collective-permute-start.6) | collective-permute-done | bytes 114720 | tf_op jit(solution)/shard_map/ppermute | solution.py:39
  46.3 11.9 %all-gather.3 = s32[4,1,8]{2,1,0:T(1,128)S(1)} all-gather(s32[1,1,8]{2,1,0:T(1,128)S(1)} %bitcast.32), channel_id=1, replica_groups=mesh['dp'=4,'vocab'=8] {'dp'}, dimensions={0}, use_global_device_ids=true | all-gather | bytes 160 | tf_op jit(solution)/shard_map/all_gather | solution.py:34
  58.2 8.0 %all-gather.4 = s32[4,1,8]{2,1,0:T(1,128)S(1)} all-gather(s32[1,1,8]{2,1,0:T(1,128)S(1)} %bitcast.33), channel_id=1, replica_groups=mesh['dp'=4,'vocab'=8] {'dp'}, dimensions={0}, use_global_device_ids=true | all-gather | bytes 160 | tf_op jit(solution)/shard_map/all_gather | solution.py:35
  66.2 13.8 %all_gather.36 = s32[32,14]{1,0:T(8,128)S(1)} all-gather(s32[8,14]{1,0:T(8,128)S(1)} %copy-done.1), channel_id=1, replica_groups=mesh['dp'=4,'vocab'=8] {'dp'}, dimensions={0}, use_global_device_ids=true | all-gather | bytes 2240 | tf_op jit(solution)/shard_map/all_gather | solution.py:59
  82.5 37.4 %all-gather.7.cloned.1.call-done = bf16[32,14,4096]{2,0,1:T(8,128)(2,1)} async-done(((bf16[8,14,4096]{2,0,1:T(8,128)(2,1)}), bf16[32,14,4096]{2,0,1:T(8,128)(2,1)}) %all-gather.7.cloned.1.call-update) | async-done | bytes 3670032 | tf_op jit(solution)/shard_map/all_gather | solution.py:58
  119.8 6.0 %copy.13 = bf16[32,14,4096]{2,1,0:T(8,128)(2,1)} copy(bf16[32,14,4096]{2,0,1:T(8,128)(2,1)} %all-gather.7.cloned.1.call-done) | data formatting | bytes 7340032 | tf_op jit(solution)/shard_map/all_gather | solution.py:58
  125.8 5.0 %reshape.122 = bf16[448,4096]{1,0:T(8,128)(2,1)} reshape(bf16[32,14,4096]{2,1,0:T(8,128)(2,1)} %copy.13) | data formatting | bytes 7340032 | tf_op jit(solution)/shard_map/reshape | solution.py:62
  130.8 5.5 %fusion.11 = (f32[448]{0:T(512)S(1)}, f32[448,501]{1,0:T(8,128)S(1)}) fusion(bf16[448,4096]{1,0:T(8,128)(2,1)} %reshape.122, bf16[4096,501]{0,1:T(8,128)(2,1)} %param.9), kind=kOutput, calls=%fused_computation.51 | convolution fusion | flops 1838902016 | bytes 8673792 | tf_op jit(solution)/shard_map/dot_general | solution.py:63
  136.7 3.2 %gather_fusion.2 = f32[448]{0:T(512)S(1)} fusion(f32[448]{0:T(512)S(1)} %get-tuple-element.45, s32[1024]{0:T(1024)S(1)} %pad_clamp_fusion), kind=kCustom, calls=%fused_computation.2 | custom fusion | bytes 5376 | tf_op jit(solution)/shard_map/gather | solution.py:76
  140.6 3.2 %all-to-all-start.2 = ((f32[4,1,112]{2,1,0:T(1,128)}), f32[4,1,112]{2,1,0:T(1,128)S(1)}, u32[]{:S(2)}, u32[]{:S(2)}) async-start(f32[4,1,112]{2,1,0:T(1,128)} %all_to_all.28), calls=%async_computation.2 | async-start | bytes 4096 | tf_op jit(solution)/shard_map/all_to_all | solution.py:80
  143.8 3.2 %gather_fusion = f32[448]{0:T(512)S(1)} fusion(f32[448]{0:T(512)S(1)} %get-tuple-element.74, s32[1024]{0:T(1024)S(1)} %pad_clamp_fusion), kind=kCustom, calls=%fused_computation | custom fusion | bytes 5376 | tf_op jit(solution)/shard_map/gather | solution.py:74
  147.7 1.6 all-to-all-done.2
  149.2 3.5 %all-to-all-start = ((f32[4,1,112]{2,1,0:T(1,128)}), f32[4,1,112]{2,1,0:T(1,128)S(1)}, u32[]{:S(2)}, u32[]{:S(2)}) async-start(f32[4,1,112]{2,1,0:T(1,128)} %all_to_all.22), calls=%async_computation | async-start | bytes 4096 | tf_op jit(solution)/shard_map/all_to_all | solution.py:78
  152.7 3.2 %gather_fusion.1 = f32[448]{0:T(512)S(1)} fusion(f32[448]{0:T(512)S(1)} %get-tuple-element.46, s32[1024]{0:T(1024)S(1)} %pad_clamp_fusion), kind=kCustom, calls=%fused_computation.1 | custom fusion | bytes 5376 | tf_op jit(solution)/shard_map/gather | solution.py:75
  156.6 1.7 all-to-all-done
  158.2 3.4 %all-to-all-start.1 = ((f32[4,1,112]{2,1,0:T(1,128)}), f32[4,1,112]{2,1,0:T(1,128)S(1)}, u32[]{:S(2)}, u32[]{:S(2)}) async-start(f32[4,1,112]{2,1,0:T(1,128)} %all_to_all.24), calls=%async_computation.1 | async-start | bytes 4096 | tf_op jit(solution)/shard_map/all_to_all | solution.py:79
  164.2 2.9 %all-to-all-done.1 = f32[4,1,112]{2,1,0:T(1,128)S(1)} async-done(((f32[4,1,112]{2,1,0:T(1,128)}), f32[4,1,112]{2,1,0:T(1,128)S(1)}, u32[]{:S(2)}, u32[]{:S(2)}) %all-to-all-start.1) | async-done | bytes 1824 | tf_op jit(solution)/shard_map/all_to_all | solution.py:79
  167.4 22.3 %all-reduce.3 = (f32[896]{0:T(1024)S(1)}, f32[896]{0:T(1024)S(1)}, f32[896]{0:T(1024)S(1)}) all-reduce(f32[896]{0:T(1024)S(1)} %dynamic-update-slice, f32[896]{0:T(1024)S(1)} %dynamic-update-slice.1, f32[896]{0:T(1024)S(1)} %dynamic-update-slice.2), channel_id=2, replica_groups=mesh['dp'=4,'vocab'=8] {'vocab'}, use_global_device_ids=true, to_apply=%add | all-reduce | flops 2688 | bytes 21504
  (88 shorter events, 12.7 us)
Async XLA Ops:
  7.2 38.1 %copy-start = (bf16[8,14,512]{2,0,1:T(8,128)(2,1)S(1)}, bf16[8,14,512]{2,0,1:T(8,128)(2,1)}, u32[]{:S(2)}) copy-start(bf16[8,14,512]{2,0,1:T(8,128)(2,1)} %param.8) | copy-start | bytes 344068
  7.2 112.7 %all-gather.7.cloned.1.call-start = ((), (), s32[]{:S(2)}) async-start(), calls=%async_computation.3 | async-start | bytes 4587520 | tf_op jit(solution)/shard_map/all_gather | solution.py:58
  7.2 6.1 %collective-permute-start = (bf16[8,14,512]{2,0,1:T(8,128)(2,1)}, bf16[8,14,512]{2,0,1:T(8,128)(2,1)S(1)}, u32[]{:S(2)}, u32[]{:S(2)}) collective-permute-start(bf16[8,14,512]{2,0,1:T(8,128)(2,1)} %param.8), channel_id=1, source_target_pairs={{0,1},{1,2},{2,3},{3,4},{4,5},{5,6},{6,7},{7,0},{8,9},{9,10},{10,1... | collective-permute-start | bytes 344072 | tf_op jit(solution)/shard_map/ppermute | solution.py:39
  13.3 5.1 %collective-permute-start.1 = (bf16[8,14,512]{2,0,1:T(8,128)(2,1)S(1)}, bf16[8,14,512]{2,0,1:T(8,128)(2,1)S(1)}, u32[]{:S(2)}, u32[]{:S(2)}) collective-permute-start(bf16[8,14,512]{2,0,1:T(8,128)(2,1)S(1)} %collective-permute-done), channel_id=1, source_target_pairs={{0,1},{1,2},{2,3},{3,4},{4,5},{5,6},{6,7},{7,0},{8,9},{9,10},{10,1... | collective-permute-start | bytes 344072 | tf_op jit(solution)/shard_map/ppermute | solution.py:39
  18.4 5.1 %collective-permute-start.2 = (bf16[8,14,512]{2,0,1:T(8,128)(2,1)S(1)}, bf16[8,14,512]{2,0,1:T(8,128)(2,1)S(1)}, u32[]{:S(2)}, u32[]{:S(2)}) collective-permute-start(bf16[8,14,512]{2,0,1:T(8,128)(2,1)S(1)} %collective-permute-done.1), channel_id=1, source_target_pairs={{0,1},{1,2},{2,3},{3,4},{4,5},{5,6},{6,7},{7,0},{8,9},{9,10},{10,1... | collective-permute-start | bytes 344072 | tf_op jit(solution)/shard_map/ppermute | solution.py:39
  23.6 5.1 %collective-permute-start.3 = (bf16[8,14,512]{2,0,1:T(8,128)(2,1)S(1)}, bf16[8,14,512]{2,0,1:T(8,128)(2,1)S(1)}, u32[]{:S(2)}, u32[]{:S(2)}) collective-permute-start(bf16[8,14,512]{2,0,1:T(8,128)(2,1)S(1)} %collective-permute-done.2), channel_id=1, source_target_pairs={{0,1},{1,2},{2,3},{3,4},{4,5},{5,6},{6,7},{7,0},{8,9},{9,10},{10,1... | collective-permute-start | bytes 344072 | tf_op jit(solution)/shard_map/ppermute | solution.py:39
  28.7 5.1 %collective-permute-start.4 = (bf16[8,14,512]{2,0,1:T(8,128)(2,1)S(1)}, bf16[8,14,512]{2,0,1:T(8,128)(2,1)S(1)}, u32[]{:S(2)}, u32[]{:S(2)}) collective-permute-start(bf16[8,14,512]{2,0,1:T(8,128)(2,1)S(1)} %collective-permute-done.3), channel_id=1, source_target_pairs={{0,1},{1,2},{2,3},{3,4},{4,5},{5,6},{6,7},{7,0},{8,9},{9,10},{10,1... | collective-permute-start | bytes 344072 | tf_op jit(solution)/shard_map/ppermute | solution.py:39
  33.8 5.1 %collective-permute-start.5 = (bf16[8,14,512]{2,0,1:T(8,128)(2,1)S(1)}, bf16[8,14,512]{2,0,1:T(8,128)(2,1)S(1)}, u32[]{:S(2)}, u32[]{:S(2)}) collective-permute-start(bf16[8,14,512]{2,0,1:T(8,128)(2,1)S(1)} %collective-permute-done.4), channel_id=1, source_target_pairs={{0,1},{1,2},{2,3},{3,4},{4,5},{5,6},{6,7},{7,0},{8,9},{9,10},{10,1... | collective-permute-start | bytes 344072 | tf_op jit(solution)/shard_map/ppermute | solution.py:39
  38.9 5.1 %collective-permute-start.6 = (bf16[8,14,512]{2,0,1:T(8,128)(2,1)S(1)}, bf16[8,14,512]{2,0,1:T(8,128)(2,1)S(1)}, u32[]{:S(2)}, u32[]{:S(2)}) collective-permute-start(bf16[8,14,512]{2,0,1:T(8,128)(2,1)S(1)} %collective-permute-done.5), channel_id=1, source_target_pairs={{0,1},{1,2},{2,3},{3,4},{4,5},{5,6},{6,7},{7,0},{8,9},{9,10},{10,1... | collective-permute-start | bytes 344072 | tf_op jit(solution)/shard_map/ppermute | solution.py:39
  45.1 1.2 copy-start.2
  45.1 13.1 %copy-start.3 = (s32[1,8]{1,0:T(1,128)S(1)}, s32[1,8]{1,0:T(1,128)}, u32[]{:S(2)}) copy-start(s32[1,8]{1,0:T(1,128)} %param.12) | copy-start | bytes 100
  45.1 21.0 %copy-start.1 = (s32[8,14]{1,0:T(8,128)S(1)}, s32[8,14]{1,0:T(8,128)}, u32[]{:S(2)}) copy-start(s32[8,14]{1,0:T(8,128)} %param.10) | copy-start | bytes 1348
  45.2 36.9 %copy-start.4 = (s32[32]{0:T(128)S(1)}, s32[32]{0:T(128)}, u32[]{:S(2)}) copy-start(s32[32]{0:T(128)} %param.13) | copy-start | bytes 388
  140.6 8.6 %all-to-all-start.2 = ((f32[4,1,112]{2,1,0:T(1,128)}), f32[4,1,112]{2,1,0:T(1,128)S(1)}, u32[]{:S(2)}, u32[]{:S(2)}) async-start(f32[4,1,112]{2,1,0:T(1,128)} %all_to_all.28), calls=%async_computation.2 | async-start | bytes 4096 | tf_op jit(solution)/shard_map/all_to_all | solution.py:80
  149.2 9.0 %all-to-all-start = ((f32[4,1,112]{2,1,0:T(1,128)}), f32[4,1,112]{2,1,0:T(1,128)S(1)}, u32[]{:S(2)}, u32[]{:S(2)}) async-start(f32[4,1,112]{2,1,0:T(1,128)} %all_to_all.22), calls=%async_computation | async-start | bytes 4096 | tf_op jit(solution)/shard_map/all_to_all | solution.py:78
  152.7 9.7 %copy-start.5 = (u32[32]{0:T(128)S(1)}, u32[32]{0:T(128)}, u32[]{:S(2)}) copy-start(u32[32]{0:T(128)} %constant.69) | copy-start | bytes 388
  158.2 8.9 %all-to-all-start.1 = ((f32[4,1,112]{2,1,0:T(1,128)}), f32[4,1,112]{2,1,0:T(1,128)S(1)}, u32[]{:S(2)}, u32[]{:S(2)}) async-start(f32[4,1,112]{2,1,0:T(1,128)} %all_to_all.24), calls=%async_computation.1 | async-start | bytes 4096 | tf_op jit(solution)/shard_map/all_to_all | solution.py:79
Sparse Core Ops, SparseCore 0:
  46.4 73.4 all-gather.6
